TPU v7x, 64 devices: a 2x2x8 block of a 4x4x8 slice. The times are simulated.
64 devices in a mesh: dp: 8 (over x, y, core), tp: 8 (over z).
Axes of the slice: x: 2, y: 2, z: 8, core: 2. Of those that a mesh axis runs over, the one named last changes fastest.
The devices are a block of a 4x4x8 slice.
Arguments:
- x: bfloat16 [18432, 3840], P(('dp', 'tp')), parts along dimension 0
- w_gate: bfloat16 [3840, 15360], P(None, 'tp')
- w_up: bfloat16 [3840, 15360], P(None, 'tp')
- w_down: bfloat16 [15360, 3840], P('tp')
Outputs:
- output: bfloat16 [18432, 3840], P(('dp', 'tp')), parts along dimension 0
There are 8 independent parts. A program takes and returns all parts, laid end to end along the dimension named above; an argument that names none is the same for every part.
All inputs are finite; a program needn't handle non-finite values.
Results may differ from a plain program's by a relative error of at most 0.016.
Values are sent between devices in bfloat16 or wider.
A program may use at most 768 MiB of HBM per device.

v0:
```python
import jax
import jax.numpy as jnp
from jax import lax
from jax.sharding import PartitionSpec as P


def solution(mesh):
    def step(x, w_gate, w_up, w_down):
        rows = lax.all_gather(x, "tp", axis=0, tiled=True)
        gate = jnp.dot(rows, w_gate, preferred_element_type=jnp.float32)
        up = jnp.dot(rows, w_up, preferred_element_type=jnp.float32)
        hidden = (jax.nn.gelu(gate) * up).astype(jnp.bfloat16)
        term = jnp.dot(hidden, w_down, preferred_element_type=jnp.float32).astype(jnp.bfloat16)
        return lax.psum_scatter(term, "tp", scatter_dimension=0, tiled=True)

    return jax.shard_map(
        step,
        mesh=mesh,
        in_specs=(P(("dp", "tp"), None), P(None, "tp"), P(None, "tp"), P("tp", None)),
        out_specs=P(("dp", "tp"), None),
        check_vma=False,
    )
```

profile of v0, /device:TPU:22, one launch (start us, length us, event | category | flops | bytes accessed | tf_op | source)
XLA Modules:
  0.0 508.6 jit_solution(10842407161898876829)
XLA Ops:
  6.5 0.0 all-gather.2.cloned.1.call-start
  6.6 0.7 all-gather.2.cloned.1.call-update
  7.3 0.1 reduce-scatter.2.cloned.1.call-start
  7.4 183.3 %all-gather.2.cloned.1.call-done = bf16[2304,3840]{1,0:T(8,128)(2,1)} async-done(((bf16[288,3840]{1,0:T(8,128)(2,1)}), bf16[2304,3840]{1,0:T(8,128)(2,1)}) %all-gather.2.cloned.1.call-update) | async-done | bytes 17694736 | tf_op jit(solution)/shard_map/all_gather | solution.py:9
  190.6 0.0 slice-start
  190.6 0.0 slice-start.1
  190.6 45.4 %fusion.9 = f32[2304,1920]{1,0:T(8,128)} fusion(bf16[2304,3840]{1,0:T(8,128)(2,1)} %all-gather.2.cloned.1.call-done, bf16[3840,1920]{1,0:T(8,128)(2,1)} %param.5), kind=kOutput, calls=%fused_computation.11 | convolution fusion | flops 33973862400 | bytes 50135040 | tf_op jit(solution)/shard_map/dot_general | solution.py:10
  236.0 0.0 slice-start.2
  236.0 0.0 slice-start.3
  236.0 46.6 %fusion.8 = bf16[2304,1920]{1,0:T(8,128)(2,1)} fusion(f32[2304,1920]{1,0:T(8,128)} %fusion.9, bf16[2304,3840]{1,0:T(8,128)(2,1)} %all-gather.2.cloned.1.call-done, bf16[3840,1920]{1,0:T(8,128)(2,1)} %param.6), kind=kOutput, calls=%fused_computation.10 | convolution fusion | flops 34018099200 | bytes 58982400 | tf_op jit(solution)/shard_map/dot_general | solution.py:11
  282.6 0.0 slice-done
  282.6 0.0 slice-done.1
  282.7 0.0 slice-done.2
  282.7 0.0 slice-done.3
  282.7 41.4 %convolution_convert_fusion = bf16[2304,3840]{1,0:T(8,128)(2,1)} fusion(bf16[2304,1920]{1,0:T(8,128)(2,1)} %fusion.8, bf16[1920,3840]{1,0:T(8,128)(2,1)S(1)} %bitcast.7), kind=kOutput, calls=%fused_computation.1 | convolution fusion | flops 33982709760 | bytes 41287680 | tf_op jit(solution)/shard_map/dot_general | solution.py:13
  324.1 0.1 reduce-scatter.2.cloned.1.call-update
  324.1 177.6 %reduce-scatter.2.cloned.1.call-done = bf16[288,3840]{1,0:T(8,128)(2,1)} async-done(((bf16[2304,3840]{1,0:T(8,128)(2,1)}), bf16[288,3840]{1,0:T(8,128)(2,1)}) %reduce-scatter.2.cloned.1.call-update) | async-done | bytes 2211856 | tf_op jit(solution)/shard_map/reduce_scatter | solution.py:14
  (1 shorter events, 0.0 us)
Async XLA Ops:
  6.5 184.1 %all-gather.2.cloned.1.call-start = ((), (), s32[]{:S(2)}) async-start(), calls=%async_computation.1 | async-start | bytes 19906560 | tf_op jit(solution)/shard_map/all_gather | solution.py:9
  7.3 494.5 %reduce-scatter.2.cloned.1.call-start = ((), (), s32[]{:S(2)}) async-start(), calls=%async_computation.2 | async-start | bytes 19906560 | tf_op jit(solution)/shard_map/reduce_scatter | solution.py:14
  190.6 92.0 %slice-start = ((s8[14745600]{0:T(1024)(128)(4,1)}), s8[4194304]{0:T(1024)(128)(4,1)S(1)}, s32[]{:S(2)}) async-start(s8[14745600]{0:T(1024)(128)(4,1)} %bitcast.6), calls=%async_computation.3 | async-start | bytes 8388608
  190.6 92.0 %slice-start.1 = ((s8[14745600]{0:T(1024)(128)(4,1)}), s8[2162688]{0:T(1024)(128)(4,1)S(1)}, s32[]{:S(2)}) async-start(s8[14745600]{0:T(1024)(128)(4,1)} %bitcast.6), calls=%async_computation.4 | async-start | bytes 4325376
  236.0 46.6 %slice-start.2 = ((s8[14745600]{0:T(1024)(128)(4,1)}), s8[4194304]{0:T(1024)(128)(4,1)S(1)}, s32[]{:S(2)}) async-start(s8[14745600]{0:T(1024)(128)(4,1)} %bitcast.6), calls=%async_computation.5 | async-start | bytes 8388608
  236.0 46.6 %slice-start.3 = ((s8[14745600]{0:T(1024)(128)(4,1)}), s8[4194304]{0:T(1024)(128)(4,1)S(1)}, s32[]{:S(2)}) async-start(s8[14745600]{0:T(1024)(128)(4,1)} %bitcast.6), calls=%async_computation.6 | async-start | bytes 8388608
Sparse Core Ops, SparseCore 0:
  8.9 181.6 all-gather.1
  324.3 177.4 reduce-scatter.1
where the time goes:
time: 509 us
  waiting for transfers between devices  362 us (71%)
  matrix products  133 us (26%)
  between operations  13.5 us (3%)
    all_gather x1, waiting for transfers between devices, step(): rows = lax.all_gather(x, 'tp', axis=0, tiled=True)  183 us
    reduce_scatter x1, waiting for transfers between devices, step(): return lax.psum_scatter(term, 'tp', scatter_dimension=0, tiled=True)  178 us
    dot_general x1, matrix products, step(): up = jnp.dot(rows, w_up, preferred_element_type=jnp.float32)  46.6 us
    dot_general x1, matrix products, step(): gate = jnp.dot(rows, w_gate, preferred_element_type=jnp.float32)  45.4 us
    dot_general x1, matrix products, step(): jnp.dot(hidden, w_down, preferred_element_type=jnp.float32)  41.4 us
  transfers between devices with their start and end apart: 2, of which 2 were waited for; matrix products, arithmetic and copies ran while one was open for 0% of the time, Pallas kernels for 0%

commit v1 on v0

v1 whole, which is shorter than its diff:
```python
import functools

import jax
import jax.numpy as jnp
from jax import lax
from jax.experimental import pallas as pl
from jax.experimental.pallas import tpu as pltpu
from jax.sharding import PartitionSpec as P

MESH = pl.DeviceIdType.MESH
F32 = jnp.float32
BF16 = jnp.bfloat16
CHUNKS = 3
TILE = 256
PAIR = (5, 7, 3, 6, 1, 4, 2)
LONG = (False, True, False, True, False, True, True)
FROM = (None, None, 0, 1, 2, 3, 5)


def kernel(n, x, wg, wu, wd, y, gx, wgv, wuv, wdv, hid, xv, stage, first, total,
           w_sem, x_sem, ag_send, ag_recv, rs_send, rs_recv, free):
    me = lax.axis_index("tp")
    right, left = {"tp": lax.rem(me + 1, n)}, {"tp": lax.rem(me + n - 1, n)}
    half = x.shape[0] // 2
    depth, width = wgv.shape
    cols = x.shape[1] // CHUNKS

    wcopies = [pltpu.make_async_copy(a, b, w_sem.at[i]) for i, (a, b) in enumerate(((wg, wgv), (wu, wuv), (wd, wdv)))]

    barrier = pltpu.get_barrier_semaphore()
    for neighbour in (left, right):
        pl.semaphore_signal(barrier, inc=1, device_id=neighbour, device_id_type=MESH)
    pl.semaphore_wait(barrier, 2)

    def ag(k, d, own=False):
        at = pl.multiple_of(lax.rem(k + 1 + d, 2) * half, half)
        src = x.at[pl.ds(at, half)] if own else gx.at[lax.rem(k + n - 4, n - 1), pl.ds(at, half)]
        return pltpu.make_async_remote_copy(
            src_ref=src, dst_ref=gx.at[k - 1, pl.ds(at, half)], send_sem=ag_send.at[d, k - 1], recv_sem=ag_recv.at[d, k - 1],
            device_id=(right, left)[d], device_id_type=MESH)

    for k in (1, 2):
        for d in (0, 1):
            ag(jnp.int32(k), d, own=True).start()
    for c in wcopies:
        c.start()

    def hidden_of(k):
        def tile(at, size):
            gate = jnp.dot(xv[...], wgv[:, pl.ds(at, size)], preferred_element_type=F32)
            up = jnp.dot(xv[...], wuv[:, pl.ds(at, size)], preferred_element_type=F32)
            hid[k, :, pl.ds(at, size)] = (jax.nn.gelu(gate) * up).astype(BF16)

        @pl.loop(0, width // TILE)
        def _(t):
            tile(pl.multiple_of(t * TILE, TILE), TILE)

        if width % TILE:
            tile(width - width % TILE, width % TILE)

    def gather_step(k):
        for d in (0, 1):
            ag(k, d).wait_recv()

        @pl.when(k <= 5)
        def _():
            for d in (0, 1):
                ag(k + 2, d).start()

        load = pltpu.make_async_copy(gx.at[k - 1], xv, x_sem)
        load.start()
        load.wait()
        hidden_of(k)

    def rs(j, c, h):
        if j == 0:
            dst = first.at[h, c]
        else:
            at = pl.multiple_of(((j - 1) * CHUNKS + c) * half, half)
            dst = (wgv, wuv)[h].at[pl.ds(at, half), pl.ds(0, cols)]
        to_right = (h == 0) == LONG[j]
        return pltpu.make_async_remote_copy(
            src_ref=stage.at[j % 2, c, pl.ds(h * half, half)], dst_ref=dst,
            send_sem=rs_send.at[h, j, c], recv_sem=rs_recv.at[h, j, c],
            device_id=right if to_right else left, device_id_type=MESH)

    def landed(j, c, h, at):
        if j == 0:
            return first[h, c, :, pl.ds(at, TILE)].astype(F32)
        row = pl.multiple_of(((j - 1) * CHUNKS + c) * half, half)
        return (wgv, wuv)[h][pl.ds(row, half), pl.ds(at, TILE)].astype(F32)

    def term(k, c, at):
        return jnp.dot(hid[k], wdv[:, pl.ds(pl.multiple_of(c * cols + at, TILE), TILE)], preferred_element_type=F32)

    def sum_step(j):
        @pl.loop(0, CHUNKS)
        def _(c):
            if FROM[j] is not None:
                for h in (0, 1):
                    rs(FROM[j], c, h).wait_recv()
            if j >= 2:
                for h in (0, 1):
                    rs(j - 2, c, h).wait_send()

            @pl.loop(0, cols // TILE)
            def _(t):
                at = pl.multiple_of(t * TILE, TILE)
                acc = term(PAIR[j], c, at)
                for h in (0, 1):
                    part = acc[h * half:(h + 1) * half]
                    if FROM[j] is not None:
                        part = part + landed(FROM[j], c, h, at)
                    stage[j % 2, c, pl.ds(h * half, half), pl.ds(at, TILE)] = part.astype(BF16)

            for h in (0, 1):
                rs(j, c, h).start()

    own = pltpu.make_async_copy(x, xv, x_sem)
    own.start()
    own.wait()
    wcopies[0].wait()
    wcopies[1].wait()
    hidden_of(0)
    pl.loop(1, 6)(gather_step)
    wcopies[2].wait()
    sum_step(0)
    pl.loop(6, 8)(gather_step)
    pl.semaphore_signal(free.at[1], inc=1, device_id=right, device_id_type=MESH)
    pl.semaphore_signal(free.at[0], inc=1, device_id=left, device_id_type=MESH)
    pl.semaphore_wait(free.at[0], 1)
    pl.semaphore_wait(free.at[1], 1)
    for j in range(1, 7):
        sum_step(j)

    @pl.loop(0, CHUNKS)
    def _(c):
        for h in (0, 1):
            rs(4, c, h).wait_recv()

        @pl.loop(0, cols // TILE)
        def _(t):
            at = pl.multiple_of(t * TILE, TILE)
            acc = term(0, c, at)
            for h in (0, 1):
                total[pl.ds(h * half, half), pl.ds(at, TILE)] = acc[h * half:(h + 1) * half] + landed(4, c, h, at)

        for h in (0, 1):
            rs(6, c, h).wait_recv()

        @pl.loop(0, cols // TILE)
        def _(t):
            at = pl.multiple_of(t * TILE, TILE)
            for h in (0, 1):
                rows = pl.ds(h * half, half)
                y[rows, pl.ds(pl.multiple_of(c * cols + at, TILE), TILE)] = (
                    total[rows, pl.ds(at, TILE)] + landed(6, c, h, at)).astype(BF16)

    @pl.loop(0, CHUNKS)
    def _(c):
        for h in (0, 1):
            rs(5, c, h).wait_send()
            rs(6, c, h).wait_send()

    @pl.loop(1, 8)
    def _(k):
        for d in (0, 1):
            ag(k, d).wait_send()


def solution(mesh):
    n = mesh.shape["tp"]

    def step(x, w_gate, w_up, w_down):
        rows, d = x.shape
        width = w_gate.shape[1]
        half, cols = rows // 2, d // CHUNKS
        dma = pltpu.SemaphoreType.DMA
        y, _ = pl.pallas_call(
            functools.partial(kernel, n),
            out_shape=(pltpu.VMEM((rows, d), BF16), jax.ShapeDtypeStruct((n - 1, rows, d), BF16)),
            in_specs=[pl.BlockSpec(memory_space=pl.ANY)] * 4,
            out_specs=(pl.BlockSpec(memory_space=pltpu.VMEM), pl.BlockSpec(memory_space=pl.ANY)),
            scratch_shapes=[
                pltpu.VMEM((d, width), BF16),
                pltpu.VMEM((d, width), BF16),
                pltpu.VMEM((width, d), BF16),
                pltpu.VMEM((n, rows, width), BF16),
                pltpu.VMEM((rows, d), BF16),
                pltpu.VMEM((2, CHUNKS, rows, cols), BF16),
                pltpu.VMEM((2, CHUNKS, half, cols), BF16),
                pltpu.VMEM((rows, cols), F32),
                dma((3,)),
                dma,
                dma((2, n - 1)),
                dma((2, n - 1)),
                dma((2, 7, CHUNKS)),
                dma((2, 7, CHUNKS)),
                pltpu.SemaphoreType.REGULAR((2,)),
            ],
            compiler_params=pltpu.CompilerParams(
                collective_id=0, has_side_effects=True, vmem_limit_bytes=67043328 - 2 * rows * d),
            cost_estimate=pl.CostEstimate(
                flops=6 * n * rows * d * width, bytes_accessed=6 * d * width + 4 * n * rows * d, transcendentals=n * rows * width),
        )(x, w_gate, w_up, w_down)
        return y

    return jax.shard_map(
        step,
        mesh=mesh,
        in_specs=(P(("dp", "tp"), None), P(None, "tp"), P(None, "tp"), P("tp", None)),
        out_specs=P(("dp", "tp"), None),
        check_vma=False,
    )
```

time: 509 us -> 343 us (0.67)
  waiting for transfers between devices: 362 us -> 0 us
  Pallas kernels: 0 us -> 342 us
  matrix products: 133 us -> 0 us
  between operations: 13.5 us -> 0.01 us
    pallas_call x0 -> x1, Pallas kernels: none -> 342 us  [step(): pl.pallas_call(functools.partial(kernel, n), out_shape=(pltpu.VMEM((rows,...]
    all_gather x1 -> x0, waiting for transfers between devices: 183 us -> none  [step(): rows = lax.all_gather(x, 'tp', axis=0, tiled=True)]
    reduce_scatter x1 -> x0, waiting for transfers between devices: 178 us -> none  [step(): return lax.psum_scatter(term, 'tp', scatter_dimension=0, tiled=True)]
    dot_general x3 -> x0, matrix products: 133 us -> none  [the longest x1 46.6 us: step(): up = jnp.dot(rows, w_up, preferred_element_type=jnp.float32)]
  transfers between devices with their start and end apart: 2 -> 0, of which waited for: 2 -> 0; matrix products, arithmetic and copies ran while one was open for 0% -> 0% of each run, Pallas kernels for 0% -> 0%
where the time goes in v1:
time: 343 us
  Pallas kernels  342 us (100%)
    pallas_call x1, Pallas kernels, step(): pl.pallas_call(functools.partial(kernel, n), out_shape=(pltpu.VMEM((rows,...  342 us

profile of v1, /device:TPU:22, one launch (start us, length us, event | category | flops | bytes accessed | tf_op | source)
XLA Modules:
  0.0 343.0 jit_solution(6244732731639425294)
XLA Ops:
  0.0 341.6 %shard_map.46 = (bf16[288,3840]{1,0:T(8,128)(2,1)S(1)}, bf16[7,288,3840]{2,1,0:T(8,128)(2,1)}) custom-call(bf16[288,3840]{1,0:T(8,128)(2,1)} %x.1, bf16[3840,1920]{1,0:T(8,128)(2,1)} %wg.1, bf16[3840,1920]{1,0:T(8,128)(2,1)} %wu.1, bf16[1920,3840]{1,0:T(8,128)(2,1)} %wd.1), custom_call_target="tpu_custom_call" | custom-call | flops 101921587200 | bytes 79626240 | tf_op jit(solution)/shard_map/pallas_call | solution.py:179
  341.7 1.4 copy.6

commit v2 on v1

--- a/solution.py
+++ b/solution.py
@@ -11,6 +11,7 @@
 F32 = jnp.float32
 BF16 = jnp.bfloat16
 CHUNKS = 3
+SHIFT = 16, 1024
 TILE = 256
 PAIR = (5, 7, 3, 6, 1, 4, 2)
 LONG = (False, True, False, True, False, True, True)
@@ -18,7 +19,7 @@
 
 
 def kernel(n, x, wg, wu, wd, y, gx, wgv, wuv, wdv, hid, xv, stage, first, total,
-           w_sem, x_sem, ag_send, ag_recv, rs_send, rs_recv, free):
+           w_sem, x_sem, ag_send, ag_recv, last_send, last_recv, rs_send, rs_recv, free):
     me = lax.axis_index("tp")
     right, left = {"tp": lax.rem(me + 1, n)}, {"tp": lax.rem(me + n - 1, n)}
     half = x.shape[0] // 2
@@ -39,6 +40,14 @@
             src_ref=src, dst_ref=gx.at[k - 1, pl.ds(at, half)], send_sem=ag_send.at[d, k - 1], recv_sem=ag_recv.at[d, k - 1],
             device_id=(right, left)[d], device_id_type=MESH)
 
+    def last(i):
+        r, c = SHIFT
+        rows = pl.ds(0, half - r) if i == 0 else pl.ds(half - r, r)
+        columns = (pl.ds(0, x.shape[1]), pl.ds(0, x.shape[1] - c), pl.ds(x.shape[1] - c, c))[i]
+        return pltpu.make_async_remote_copy(
+            src_ref=gx.at[n - 3 if i == 2 else n - 4, rows, columns], dst_ref=gx.at[n - 2, rows, columns],
+            send_sem=last_send.at[i], recv_sem=last_recv.at[i], device_id=left if i == 2 else right, device_id_type=MESH)
+
     for k in (1, 2):
         for d in (0, 1):
             ag(jnp.int32(k), d, own=True).start()
@@ -62,11 +71,24 @@
         for d in (0, 1):
             ag(k, d).wait_recv()
 
-        @pl.when(k <= 5)
+        @pl.when(k <= 4)
         def _():
             for d in (0, 1):
                 ag(k + 2, d).start()
 
+        @pl.when(k == 5)
+        def _():
+            last(0).start()
+            last(1).start()
+            ag(7, 1).start()
+
+        @pl.when(k == 6)
+        def _():
+            last(2).start()
+
+        load_hidden(k)
+
+    def load_hidden(k):
         load = pltpu.make_async_copy(gx.at[k - 1], xv, x_sem)
         load.start()
         load.wait()
@@ -122,10 +144,13 @@
     wcopies[0].wait()
     wcopies[1].wait()
     hidden_of(0)
-    pl.loop(1, 6)(gather_step)
+    pl.loop(1, 7)(gather_step)
     wcopies[2].wait()
     sum_step(0)
-    pl.loop(6, 8)(gather_step)
+    ag(7, 1).wait_recv()
+    for i in range(3):
+        last(i).wait_recv()
+    load_hidden(7)
     pl.semaphore_signal(free.at[1], inc=1, device_id=right, device_id_type=MESH)
     pl.semaphore_signal(free.at[0], inc=1, device_id=left, device_id_type=MESH)
     pl.semaphore_wait(free.at[0], 1)
@@ -162,10 +187,14 @@
             rs(5, c, h).wait_send()
             rs(6, c, h).wait_send()
 
-    @pl.loop(1, 8)
+    @pl.loop(1, 7)
     def _(k):
         for d in (0, 1):
             ag(k, d).wait_send()
+
+    ag(7, 1).wait_send()
+    for i in range(3):
+        last(i).wait_send()
 
 
 def solution(mesh):
@@ -194,6 +223,8 @@
                 dma,
                 dma((2, n - 1)),
                 dma((2, n - 1)),
+                dma((3,)),
+                dma((3,)),
                 dma((2, 7, CHUNKS)),
                 dma((2, 7, CHUNKS)),
                 pltpu.SemaphoreType.REGULAR((2,)),

time: 343 us -> 343 us (level)
  no operation moved by 1% of the time
where the time goes in v2:
time: 343 us; the launch traced here: 342 us
  Pallas kernels  341 us (99%)
    pallas_call x1, Pallas kernels, step(): pl.pallas_call(functools.partial(kernel, n), out_shape=(pltpu.VMEM((rows,...  341 us

profile of v2, /device:TPU:22, one launch (start us, length us, event | category | flops | bytes accessed | tf_op | source)
XLA Modules:
  0.0 342.4 jit_solution(6573556557727085560)
XLA Ops:
  0.0 341.0 %shard_map.46 = (bf16[288,3840]{1,0:T(8,128)(2,1)S(1)}, bf16[7,288,3840]{2,1,0:T(8,128)(2,1)}) custom-call(bf16[288,3840]{1,0:T(8,128)(2,1)} %x.1, bf16[3840,1920]{1,0:T(8,128)(2,1)} %wg.1, bf16[3840,1920]{1,0:T(8,128)(2,1)} %wu.1, bf16[1920,3840]{1,0:T(8,128)(2,1)} %wd.1), custom_call_target="tpu_custom_call" | custom-call | flops 101921587200 | bytes 79626240 | tf_op jit(solution)/shard_map/pallas_call | solution.py:208
  341.0 1.4 copy.6
